TPU v7x, 32 devices: a whole 2x2x4 slice. The times are simulated.
32 devices in a mesh: head: 4 (over y, core), row: 8 (over z, x).
Axes of the slice: x: 2, y: 2, z: 4, core: 2. Of those that a mesh axis runs over, the one named last changes fastest.
Arguments:
- hidden_in: bfloat16 [512, 2048], replicated, may hold values from -6 to 6
- w_query: bfloat16 [2048, 16, 128], P(None, 'head', 'row'), may hold values from -0.125 to 0.125
- w_key: bfloat16 [2048, 16, 128], P(None, 'head', 'row'), may hold values from -0.125 to 0.125
- w_value: bfloat16 [2048, 32, 128], P(None, 'head'), may hold values from -0.125 to 0.125
- w_zgate: bfloat16 [2048, 32, 128], P(None, 'head'), may hold values from -0.125 to 0.125
- w_decay: bfloat16 [2048, 32], P(None, 'head'), may hold values from -0.125 to 0.125
- w_beta: bfloat16 [2048, 32], P(None, 'head'), may hold values from -0.125 to 0.125
- decay_log: float32 [32], P('head'), may hold values from -1.5 to 1.5
- dt_bias: float32 [32], P('head'), may hold values from -2 to 2
- norm_gain: float32 [128], replicated, may hold values from 0.1 to 1.9
- w_out: bfloat16 [32, 128, 2048], P('head'), may hold values from -0.09375 to 0.09375
- state: float32 [512, 32, 128, 128], P(None, 'head', 'row'), may hold values from -6 to 6
Outputs:
- layer_out: bfloat16 [512, 2048], P('row', 'head')
- new_state: float32 [512, 32, 128, 128], P(None, 'head', 'row')
All inputs are finite; a program needn't handle non-finite values.
Results may differ from a plain program's by a relative error of at most 0.005.
Values sent between devices are 32-bit elements; how exact they have to be, the bound alone decides.
A program may use at most 128 MiB of HBM per device.

v0:
```python
import jax
import jax.numpy as jnp
from jax import lax
from jax.sharding import PartitionSpec as P


def local(
    hidden_in,
    w_query,
    w_key,
    w_value,
    w_zgate,
    w_decay,
    w_beta,
    decay_log,
    dt_bias,
    norm_gain,
    w_out,
    state,
):
    query = jnp.einsum("bd,dhk->bhk", hidden_in, w_query, preferred_element_type=jnp.float32)
    keys = jnp.einsum("bd,dhk->bhk", hidden_in, w_key, preferred_element_type=jnp.float32)
    values = jnp.einsum("bd,dhv->bhv", hidden_in, w_value, preferred_element_type=jnp.float32)
    decay_in = jnp.dot(hidden_in, w_decay, preferred_element_type=jnp.float32) + dt_bias
    decay = jnp.exp(-jnp.exp(decay_log) * jax.nn.softplus(decay_in))
    beta = jax.nn.sigmoid(jnp.dot(hidden_in, w_beta, preferred_element_type=jnp.float32))
    group = state.shape[1] // keys.shape[1]

    def widen(array):
        return jnp.repeat(array, group, axis=1)

    def read_state(source, vector):
        return jnp.einsum("bhkv,bhk->bhv", source, widen(vector), precision=lax.Precision.HIGHEST)

    query_sq, key_sq = lax.psum(
        (jnp.sum(query * query, axis=-1), jnp.sum(keys * keys, axis=-1)), "row"
    )
    query_unit = query * lax.rsqrt(1.0 + query_sq)[..., None]
    key_unit = keys * lax.rsqrt(1.0 + key_sq)[..., None]
    readk, readq_old, unit_dot = lax.psum(
        (
            read_state(state, key_unit),
            read_state(state, query_unit),
            jnp.sum(query_unit * key_unit, axis=-1),
        ),
        "row",
    )
    delta = beta[..., None] * (values - decay[..., None] * readk)
    new_state = decay[..., None, None] * state + widen(key_unit)[..., None] * delta[:, :, None, :]
    own_rows = hidden_in.shape[0] // lax.axis_size("row")
    first_row = lax.axis_index("row") * own_rows
    readq_all = decay[..., None] * readq_old + widen(unit_dot)[..., None] * delta
    readq = lax.dynamic_slice_in_dim(readq_all, first_row, own_rows, 0)
    own_hidden = lax.dynamic_slice_in_dim(hidden_in, first_row, own_rows, 0)
    zgate = jnp.einsum("bd,dhv->bhv", own_hidden, w_zgate, preferred_element_type=jnp.float32)
    meansq = jnp.mean(readq * readq, axis=-1, keepdims=True)
    normed = (readq * lax.rsqrt(meansq + 0.5) * norm_gain * jax.nn.silu(zgate)).astype(jnp.bfloat16)
    partial_out = jnp.einsum("bhv,hvd->bd", normed, w_out, preferred_element_type=jnp.float32)
    layer_out = lax.psum_scatter(partial_out, "head", scatter_dimension=1, tiled=True).astype(
        jnp.bfloat16
    )
    return (layer_out, new_state)


def solution(mesh):
    in_specs = (
        P(),
        P(None, "head", "row"),
        P(None, "head", "row"),
        P(None, "head", None),
        P(None, "head", None),
        P(None, "head"),
        P(None, "head"),
        P("head"),
        P("head"),
        P(),
        P("head", None, None),
        P(None, "head", "row", None),
    )
    out_specs = (P("row", "head"), P(None, "head", "row", None))
    return jax.shard_map(local, mesh=mesh, in_specs=in_specs, out_specs=out_specs, check_vma=False)
```

profile of v0, /device:TPU:0, one launch (start us, length us, event | category | flops | bytes accessed | tf_op | source)
XLA Modules:
  0.0 326.1 jit_solution(11557433806392551255)
XLA Ops:
  7.2 0.0 copy-start
  7.2 0.0 copy-start.3
  7.2 0.0 all-reduce.4.cloned.1.call-start
  7.2 1.5 copy-done
  8.8 1.7 multiply_reduce_fusion.3
  10.5 0.0 copy-done.3
  10.5 0.8 multiply_reduce_fusion.2
  11.3 38.8 %all-reduce = (f32[512,4]{0,1:T(4,128)S(1)}, f32[512,4]{0,1:T(4,128)S(1)}) all-reduce(f32[512,4]{0,1:T(4,128)S(1)} %get-tuple-element.9, f32[512,4]{0,1:T(4,128)S(1)} %get-tuple-element.11), channel_id=1, replica_groups=mesh['head'=4,'row'=8] {'row'}, use_global_device_ids=true, to_apply=%region_4.5 | all-reduce | flops 4096 | bytes 32768 | tf_op jit(solution)/shard_map/psum | solution.py:35
  50.1 0.1 multiply_reduce_fusion.1
  50.2 0.4 copy.21
  50.6 3.5 %copy.25 = f32[512,8,16,1]{2,3,1,0:T(1,128)} copy(f32[512,8,16,1]{0,2,1,3:T(8,128)S(1)} %bitcast.57) | data formatting | bytes 524288 | tf_op jit(solution)/shard_map/reshape | solution.py:30
  54.2 32.3 %fusion.35 = f32[512,8,1,128]{3,2,1,0:T(1,128)S(1)} fusion(f32[512,8,16,1]{2,3,1,0:T(1,128)} %copy.25, f32[512,8,16,128]{3,2,1,0:T(8,128)} %param.23), kind=kOutput, calls=%fused_computation.43 | convolution fusion | flops 100663296 | bytes 35913728 | tf_op jit(solution)/shard_map/bhkv,bhk->bhv/dot_general | solution.py:33
  86.5 1.7 copy.42
  88.2 0.7 broadcast_in_dim.8
  88.9 0.0 copy-start.1
  88.9 33.1 %fusion.36 = f32[512,8,1,128]{3,2,1,0:T(1,128)S(1)} fusion(f32[512,8,16,1]{2,3,1,0:T(1,128)S(1)} %bitcast.53, f32[512,8,16,128]{3,2,1,0:T(8,128)} %param.23), kind=kOutput, calls=%fused_computation.44 | convolution fusion | flops 100663296 | bytes 35913728 | tf_op jit(solution)/shard_map/bhkv,bhk->bhv/dot_general | solution.py:33
  122.0 0.0 copy-done.1
  122.0 1.7 copy.41
  123.7 0.0 copy-start.8
  123.7 0.0 copy-start.4
  123.7 0.0 copy-start.7
  123.7 0.0 all-reduce.4.cloned.1.call-update
  123.7 0.0 copy-start.5
  123.7 0.0 reduce-scatter.2.cloned.1.call-start
  123.8 18.4 %psum.38 = f32[512,4]{0,1:T(4,128)S(1)} all-reduce(f32[512,4]{0,1:T(4,128)S(1)} %get-tuple-element.6), channel_id=1, replica_groups=mesh['head'=4,'row'=8] {'row'}, use_global_device_ids=true, to_apply=%region_6.7 | all-reduce | flops 2048 | bytes 16384 | tf_op jit(solution)/shard_map/psum | solution.py:40
  142.3 0.0 copy-done.8
  142.3 0.0 copy-done.4
  142.3 0.0 copy-done.7
  142.3 0.7 fusion.31
  143.0 0.1 copy.23
  143.1 0.1 constant_dynamic-slice_fusion.1
  143.2 0.1 constant_dynamic-slice_fusion
  143.3 0.0 copy-done.5
  143.3 0.7 fusion.11
  144.0 134.0 %all-reduce.4.cloned.1.call-done = (f32[512,8,128]{2,0,1:T(8,128)}, f32[512,8,128]{2,0,1:T(8,128)}) async-done(((f32[512,8,128]{2,0,1:T(8,128)}, f32[512,8,128]{2,0,1:T(8,128)}), (f32[512,8,128]{2,0,1:T(8,128)}, f32[512,8,128]{2,0,1:T(8,128)})) %all-reduce.4.cloned.1.call-update) | async-done | bytes 4194320 | tf_op jit(solution)/shard_map/psum | solution.py:40
  278.0 5.2 %subtract_multiply_fusion = f32[512,8,128]{2,0,1:T(8,128)S(1)} fusion(f32[512,8,128]{2,0,1:T(8,128)} %get-tuple-element.4, bf16[2048,8,128]{2,1,0:T(8,128)(2,1)} %param.15, bf16[512,2048]{1,0:T(8,128)(2,1)S(1)} %copy-done, f32[512,8]{0,1:T(8,128)S(1)} %fusion.11, f32[512,8]{0,1:T(8,128)S(1)} %fusion.31), kind=kOutput, calls=%fused_computation.9 | convolution fusion | flops 2149056512 | bytes 10518528 | tf_op jit(solution)/shard_map/bd,dhv->bhv/dot_general | solution.py:23
  283.2 0.0 copy-start.2
  283.2 0.0 copy-start.6
  283.3 2.5 copy.24
  285.8 0.0 copy-done.2
  285.8 1.3 multiply_reduce_fusion
  287.1 0.0 copy-done.6
  287.1 6.1 %convolution_bitcast_fusion = f32[64,2048]{1,0:T(8,128)} fusion(bf16[8,128,2048]{2,1,0:T(8,128)(2,1)} %param.22, bf16[2048,8,128]{2,1,0:T(8,128)(2,1)} %param.16, bf16[512,2048]{1,0:T(8,128)(2,1)S(1)} %copy-done, s32[]{:T(128)S(6)} %select_n.9, f32[128]{0:T(128)S(1)} %copy-done.6, f32[64,8]{0,1:T(8,128)S(1)} %add_rsqrt_fusion.2, ...), kind=kOutput, calls=%fused_computation.5 | convolution fusion | flops 537591808 | bytes 9713152 | tf_op jit(solution)/shard_map/bhv,hvd->bd/dot_general | solution.py:58
  293.2 0.0 reduce-scatter.2.cloned.1.call-update
  293.2 24.5 %multiply_add_fusion = f32[512,8,16,128]{3,2,1,0:T(8,128)} fusion(f32[512,8,16,128]{3,2,1,0:T(8,128)} %param.23, f32[512,8,128]{2,1,0:T(8,128)} %copy.24, f32[512,8,16]{2,1,0:T(8,128)} %bitcast.54, f32[512,8]{1,0:T(8,128)S(1)} %copy.23), kind=kLoop, calls=%fused_computation | loop fusion | flops 25165824 | bytes 69484544 | tf_op jit(solution)/shard_map/add | solution.py:49
  317.7 0.0 reduce-scatter.2.cloned.1.call-done
  317.8 1.5 convert_element_type.7
  (6 shorter events, 0.1 us)
Async XLA Ops:
  7.2 1.6 copy-start
  7.2 3.3 %copy-start.3 = (bf16[2048,4,16]{0,2,1:T(8,128)(2,1)S(1)}, bf16[2048,4,16]{0,2,1:T(8,128)(2,1)}, u32[]{:S(2)}) copy-start(bf16[2048,4,16]{0,2,1:T(8,128)(2,1)} %param.14) | copy-start | bytes 786436
  7.2 270.8 %all-reduce.4.cloned.1.call-start = ((), (), s32[]{:S(2)}) async-start(), calls=%async_computation.2 | async-start | bytes 8388608 | tf_op jit(solution)/shard_map/psum | solution.py:40
  88.9 33.1 %copy-start.1 = (f32[512,4,2,16]{3,2,1,0:T(2,128)}, f32[512,4,2,16]{3,2,1,0:T(2,128)S(1)}, u32[]{:S(2)}) copy-start(f32[512,4,2,16]{3,2,1,0:T(2,128)S(1)} %broadcast_in_dim.8) | copy-start | bytes 786436
  123.7 18.6 %copy-start.8 = (f32[8]{0:T(128)S(1)}, f32[8]{0:T(128)}, u32[]{:S(2)}) copy-start(f32[8]{0:T(128)} %param.19) | copy-start | bytes 100
  123.7 18.6 %copy-start.4 = (bf16[2048,8]{0,1:T(8,128)(2,1)S(1)}, bf16[2048,8]{0,1:T(8,128)(2,1)}, u32[]{:S(2)}) copy-start(bf16[2048,8]{0,1:T(8,128)(2,1)} %param.17) | copy-start | bytes 98308
  123.7 18.6 %copy-start.7 = (f32[8]{0:T(128)S(1)}, f32[8]{0:T(128)}, u32[]{:S(2)}) copy-start(f32[8]{0:T(128)} %param.20) | copy-start | bytes 100
  123.7 19.6 %copy-start.5 = (bf16[2048,8]{0,1:T(8,128)(2,1)S(1)}, bf16[2048,8]{0,1:T(8,128)(2,1)}, u32[]{:S(2)}) copy-start(bf16[2048,8]{0,1:T(8,128)(2,1)} %param.18) | copy-start | bytes 98308
  123.7 194.0 %reduce-scatter.2.cloned.1.call-start = ((), (), s32[]{:S(2)}) async-start(), calls=%async_computation.1 | async-start | bytes 655360 | tf_op jit(solution)/shard_map/reduce_scatter | solution.py:59
  283.2 2.6 copy-start.2
  283.2 3.9 %copy-start.6 = (f32[128]{0:T(128)S(1)}, f32[128]{0:T(128)}, u32[]{:S(2)}) copy-start(f32[128]{0:T(128)} %param.21) | copy-start | bytes 1540
Sparse Core Ops, SparseCore 0:
  123.9 154.0 all-reduce.3
  293.3 20.6 reduce-scatter.1
where the time goes:
time: 326 us
  waiting for transfers between devices  134 us (41%)
  matrix products  80.5 us (25%)
  blocking collectives  57.3 us (18%)
  other arithmetic  27.4 us (8%)
  between operations  14.3 us (4%)
  local copies, waits for them, and re-layouts  12.5 us (4%)
    psum x1, waiting for transfers between devices, local(): lax.psum((read_state(state, key_unit), read_state(state, query_unit), jnp...  134 us
    dot_general x2, matrix products, read_state(): jnp.einsum('bhkv,bhk->bhv', source, widen(vector), precision=lax.Precisio...  65.4 us
    psum x1, blocking collectives, local(): lax.psum((jnp.sum(query * query, axis=-1), jnp.sum(keys * keys, axis=-1))...  38.8 us
    add x1, other arithmetic, local(): decay[..., None, None] * state  24.5 us
    psum x1, blocking collectives, local(): lax.psum((read_state(state, key_unit), read_state(state, query_unit), jnp...  18.4 us
  transfers between devices with their start and end apart: 2, of which 1 were waited for; matrix products, arithmetic and copies ran while one was open for 8% of the time, Pallas kernels for 0%

commit v1 on v0

v1 whole, which is shorter than its diff:
```python
import functools

import jax
import jax.numpy as jnp
from jax import lax
from jax.experimental import pallas as pl
from jax.experimental.pallas import tpu as pltpu
from jax.sharding import PartitionSpec as P

MESH = pl.DeviceIdType.MESH
F32 = jnp.float32
BF16 = jnp.bfloat16


def head_mask(heads, depth, group_rows):
    lane = lax.broadcasted_iota(jnp.int32, (group_rows, heads * depth), 1)
    row = lax.broadcasted_iota(jnp.int32, (group_rows, heads * depth), 0)
    low = row * depth
    return (lane >= low) & (lane < low + depth)


def read_kernel(heads, depth, q_ref, k_ref, s_ref, rk_ref, rq_ref):
    seqs, _, width = s_ref.shape
    mask = head_mask(heads, depth, heads)

    def body(b, carry):
        krow = jnp.broadcast_to(k_ref[pl.ds(b, 1), :], (heads, heads * depth))
        qrow = jnp.broadcast_to(q_ref[pl.ds(b, 1), :], (heads, heads * depth))
        left = jnp.concatenate([jnp.where(mask, krow, 0.0), jnp.where(mask, qrow, 0.0)], axis=0)
        read = jnp.dot(
            left.astype(BF16), s_ref[b].astype(BF16), preferred_element_type=F32
        )
        at = pl.multiple_of(b * heads, heads)
        rk_ref[pl.ds(at, heads), :] = read[:heads]
        rq_ref[pl.ds(at, heads), :] = read[heads:]
        return carry

    lax.fori_loop(0, seqs, body, 0, unroll=8)


def update_kernel(heads, depth, k_ref, decay_ref, delta_ref, s_ref, out_ref):
    seqs, _, width = s_ref.shape
    mask = head_mask(heads, depth, heads)

    def body(b, carry):
        krow = jnp.broadcast_to(k_ref[pl.ds(b, 1), :], (heads, heads * depth))
        left = jnp.where(mask, krow, 0.0).astype(BF16)
        at = pl.multiple_of(b * heads, heads)
        delta = delta_ref[pl.ds(at, heads), :].astype(BF16)
        decay = decay_ref[pl.ds(at, heads), :]
        add = lax.dot_general(
            left, delta, (((0,), (0,)), ((), ())), preferred_element_type=F32
        )
        for h in range(heads):
            rows = slice(h * depth, (h + 1) * depth)
            out_ref[b, rows, :] = decay[h : h + 1, :] * s_ref[b, rows, :] + add[rows, :]
        return carry

    lax.fori_loop(0, seqs, body, 0, unroll=8)


def exchange_kernel(
    nx, nz, nh, heads, group, own,
    rk_ref, rq_ref, stats_ref, values_ref, zgate_ref, decay_ref, beta_ref, gain_ref, wout_ref,
    delta_ref, layer_ref,
    kx, ksum, kz, ktot, qz, qsum, qx, qtot, st, normed, part, hrecv,
    kx_s, kx_r, kz_s, kz_r, qz_s, qz_r, qx_s, qx_r, st_s, st_r,
    ax_s, ax_r, az_s, az_r, bz_s, bz_r, bx_s, bx_r, h_s, h_r,
):
    me = lax.axis_index("row")
    my_head = lax.axis_index("head")
    x = lax.rem(me, nx)
    z = lax.div(me, nx)
    nrow = nx * nz
    blk = own * heads
    half = blk // 2

    def at(index, size):
        return pl.ds(pl.multiple_of(index * size, size), size)

    barrier = pltpu.get_barrier_semaphore()
    for d in range(1, nrow):
        pl.semaphore_signal(
            barrier, inc=1, device_id={"row": lax.rem(me + d, nrow)}, device_id_type=MESH
        )
    for d in range(1, nh):
        pl.semaphore_signal(
            barrier, inc=1, device_id={"head": lax.rem(my_head + d, nh)}, device_id_type=MESH
        )
    pl.semaphore_wait(barrier, nrow - 1 + nh - 1)

    def send(src, dst, ssem, rsem, row):
        copy = pltpu.make_async_remote_copy(
            src_ref=src, dst_ref=dst, send_sem=ssem, recv_sem=rsem,
            device_id={"row": row}, device_id_type=MESH,
        )
        copy.start()
        return copy

    zorder = sorted(range(nz), key=lambda d: -min(d, nz - d))
    sent = []

    stats_in = []
    for d in range(1, nrow):
        to = lax.rem(me + d, nrow)
        stats_in.append(
            send(stats_ref.at[at(to, own)], st.at[d - 1], st_s.at[d - 1], st_r.at[d - 1], to)
        )
    kx_in = {}
    for d in zorder:
        zt = lax.rem(z + d, nz)
        for e in range(1, nx):
            xt = lax.rem(x + e, nx)
            i = (e - 1) * nz + d
            kx_in[e, d] = send(
                rk_ref.at[at(zt * nx + xt, blk)], kx.at[i], kx_s.at[i], kx_r.at[i], z * nx + xt
            )
    qz_in = {}
    for d in zorder:
        if d:
            zt = lax.rem(z + d, nz)
            qz_in[d] = send(
                rq_ref.at[at(zt, nx * blk)], qz.at[d - 1], qz_s.at[d - 1], qz_r.at[d - 1],
                zt * nx + x,
            )
    kz_in = {}
    for d in zorder:
        zt = lax.rem(z + d, nz)
        total = rk_ref[at(zt * nx + x, blk), :]
        for e in range(1, nx):
            kx_in[e, d].wait_recv()
            total = total + kx[(e - 1) * nz + d]
        if d:
            ksum[d - 1] = total
            kz_in[d] = send(
                ksum.at[d - 1], kz.at[d - 1], kz_s.at[d - 1], kz_r.at[d - 1], zt * nx + x
            )
        else:
            ktot[...] = total
    stats = stats_ref[at(me, own), :]
    for d in range(1, nrow):
        stats_in[d - 1].wait_recv()
        stats = stats + st[d - 1]
    total = ktot[...]
    for d in range(1, nz):
        kz_in[d].wait_recv()
        total = total + kz[d - 1]
    ktot[...] = total

    mine = me * blk
    for h in range(heads):
        c = h // group
        kscale = lax.rsqrt(1.0 + stats[:, c : c + 1])
        cols = slice(h * 128, (h + 1) * 128)
        readk = ktot[pl.ds(h, own, stride=heads), :] * kscale
        delta = beta_ref[:, h : h + 1] * (values_ref[:, cols] - decay_ref[:, h : h + 1] * readk)
        ktot[pl.ds(h, own, stride=heads), :] = delta * kscale
    delta_ref[at(me, blk), :] = ktot[...]

    def lo(row):
        return pl.ds(pl.multiple_of(row * blk, half), half)

    def hi(row):
        return pl.ds(pl.multiple_of(row * blk + half, half), half)

    ax_in, az_in, bz_in, bx_in = {}, {}, {}, {}
    for e in range(1, nx):
        xt = lax.rem(x + e, nx)
        ax_in[e] = send(
            ktot.at[pl.ds(0, half)], delta_ref.at[lo(me)], ax_s.at[e - 1], ax_r.at[e - 1],
            z * nx + xt,
        )
    for d in zorder:
        if d:
            zt = lax.rem(z + d, nz)
            bz_in[d] = send(
                ktot.at[pl.ds(half, half)], delta_ref.at[hi(me)], bz_s.at[d - 1], bz_r.at[d - 1],
                zt * nx + x,
            )
    for d in zorder:
        if d:
            i = d - 1
            zt = lax.rem(z + d, nz)
            az_in[0, d] = send(
                ktot.at[pl.ds(0, half)], delta_ref.at[lo(me)], az_s.at[i], az_r.at[i], zt * nx + x
            )
    for e in range(1, nx):
        i = (e - 1) * nz
        xt = lax.rem(x + e, nx)
        bx_in[e, 0] = send(
            ktot.at[pl.ds(half, half)], delta_ref.at[hi(me)], bx_s.at[i], bx_r.at[i], z * nx + xt
        )
    for d in zorder:
        if d:
            qz_in[d].wait_recv()
    qx_in = {}
    for e in list(range(1, nx)) + [0]:
        xt = lax.rem(x + e, nx)
        total = rq_ref[at(z * nx + xt, blk), :]
        for d in range(1, nz):
            total = total + qz[d - 1, at(xt, blk), :]
        if e:
            qsum[e - 1] = total
            qx_in[e] = send(
                qsum.at[e - 1], qx.at[e - 1], qx_s.at[e - 1], qx_r.at[e - 1], z * nx + xt
            )
        else:
            qtot[...] = total
    for e in range(1, nx):
        ax_in[e].wait_recv()
        source = z * nx + lax.rem(x - e + nx, nx)
        for d in zorder:
            if d:
                i = e * (nz - 1) + d - 1
                zt = lax.rem(z + d, nz)
                az_in[e, d] = send(
                    delta_ref.at[lo(source)], delta_ref.at[lo(source)], az_s.at[i], az_r.at[i],
                    zt * nx + x,
                )
    for d in sorted(range(1, nz), key=lambda d: min(d, nz - d)):
        bz_in[d].wait_recv()
        source = lax.rem(z - d + nz, nz) * nx + x
        for e in range(1, nx):
            i = (e - 1) * nz + d
            xt = lax.rem(x + e, nx)
            bx_in[e, d] = send(
                delta_ref.at[hi(source)], delta_ref.at[hi(source)], bx_s.at[i], bx_r.at[i],
                z * nx + xt,
            )
    total = qtot[...]
    for e in range(1, nx):
        qx_in[e].wait_recv()
        total = total + qx[e - 1]
    qtot[...] = total
    hk = heads // group
    for h in range(heads):
        c = h // group
        kscale = lax.rsqrt(1.0 + stats[:, c : c + 1])
        qscale = lax.rsqrt(1.0 + stats[:, hk + c : hk + c + 1])
        unit = stats[:, 2 * hk + c : 2 * hk + c + 1] * qscale
        cols = slice(h * 128, (h + 1) * 128)
        readq = (
            decay_ref[:, h : h + 1] * (qtot[pl.ds(h, own, stride=heads), :] * qscale)
            + unit * ktot[pl.ds(h, own, stride=heads), :]
        )
        meansq = jnp.mean(readq * readq, axis=-1, keepdims=True)
        gate = jax.nn.silu(zgate_ref[:, cols])
        out = readq * lax.rsqrt(meansq + 0.5) * gain_ref[...] * gate
        normed[:, cols] = out.astype(BF16)
    width = layer_ref.shape[1]
    h_in = {}
    for d in list(range(1, nh)) + [0]:
        to = lax.rem(my_head + d, nh)
        part[d] = jnp.dot(
            normed[...], wout_ref[:, at(to, width)], preferred_element_type=F32
        )
        if d:
            h_in[d] = pltpu.make_async_remote_copy(
                src_ref=part.at[d], dst_ref=hrecv.at[d - 1], send_sem=h_s.at[d - 1],
                recv_sem=h_r.at[d - 1], device_id={"head": to}, device_id_type=MESH,
            )
            h_in[d].start()
    total = part[0]
    for d in range(1, nh):
        h_in[d].wait_recv()
        total = total + hrecv[d - 1]
    layer_ref[...] = total.astype(BF16)

    for group_in in (az_in, bx_in):
        for key, copy in group_in.items():
            copy.wait_recv()
    for group_in in (kx_in, qz_in, kz_in, ax_in, az_in, bz_in, bx_in, qx_in, h_in):
        for key, copy in group_in.items():
            copy.wait_send()
    for copy in stats_in:
        copy.wait_send()


def split_rows(rows):
    nx = 1
    while (2 * nx) * (2 * nx) <= rows:
        nx *= 2
    return nx, rows // nx


def local(
    hidden_in, w_query, w_key, w_value, w_zgate, w_decay, w_beta, decay_log, dt_bias,
    norm_gain, w_out, state,
):
    seqs, model = hidden_in.shape
    _, hk, depth = w_key.shape
    heads, width = state.shape[1], state.shape[3]
    group = heads // hk
    wide = heads * depth
    nrow, nh = lax.axis_size("row"), lax.axis_size("head")
    nx, nz = split_rows(nrow)
    own = seqs // nrow
    first = lax.axis_index("row") * own

    w_qk = jnp.concatenate(
        [
            jnp.repeat(w_query, group, axis=1).reshape(model, wide),
            jnp.repeat(w_key, group, axis=1).reshape(model, wide),
        ],
        axis=1,
    )
    qk = jnp.dot(hidden_in, w_qk, preferred_element_type=F32)
    query, keys = qk[:, :wide], qk[:, wide:]
    cols = jnp.arange(wide)
    pick = ((cols[:, None] // (depth * group)) == jnp.arange(hk)[None, :]) & (
        (cols[:, None] // depth) % group == 0
    )

    def head_sum(array):
        return jnp.dot(array, pick.astype(F32), precision=lax.Precision.HIGHEST)

    stats = jnp.concatenate(
        [head_sum(keys * keys), head_sum(query * query), head_sum(query * keys)], axis=1
    )
    stats = jnp.pad(stats, ((0, 0), (0, 128 - 3 * hk)))
    small = jnp.dot(
        hidden_in, jnp.concatenate([w_decay, w_beta], axis=1), preferred_element_type=F32
    )
    decay = jnp.exp(-jnp.exp(decay_log) * jax.nn.softplus(small[:, :heads] + dt_bias))
    beta = jax.nn.sigmoid(small[:, heads:])
    decay_wide = jnp.broadcast_to(decay[:, :, None], (seqs, heads, width)).reshape(-1, width)
    own_hidden = lax.dynamic_slice_in_dim(hidden_in, first, own, 0)
    own_decay = lax.dynamic_slice_in_dim(decay, first, own, 0)
    own_beta = lax.dynamic_slice_in_dim(beta, first, own, 0)
    values = jnp.einsum("bd,dhv->bhv", own_hidden, w_value, preferred_element_type=F32)
    zgate = jnp.einsum("bd,dhv->bhv", own_hidden, w_zgate, preferred_element_type=F32)

    flat = state.reshape(seqs, wide, width)
    step = 32
    row_spec = pl.BlockSpec((step, wide), lambda i: (i, 0))
    head_spec = pl.BlockSpec((step * heads, width), lambda i: (i, 0))
    state_spec = pl.BlockSpec((step, wide, width), lambda i: (i, 0, 0))
    by_head = jax.ShapeDtypeStruct((seqs * heads, width), F32)
    rk, rq = pl.pallas_call(
        functools.partial(read_kernel, heads, depth),
        grid=(seqs // step,),
        in_specs=[row_spec, row_spec, state_spec],
        out_specs=[head_spec, head_spec],
        out_shape=[by_head, by_head],
        name="read",
    )(query, keys, flat)

    blk = own * heads
    vmem = pl.BlockSpec(memory_space=pltpu.VMEM)
    dma = lambda n: pltpu.SemaphoreType.DMA((n,))
    delta, layer_out = pl.pallas_call(
        functools.partial(exchange_kernel, nx, nz, nh, heads, group, own),
        in_specs=[vmem] * 9,
        out_specs=[vmem] * 2,
        out_shape=[by_head, jax.ShapeDtypeStruct((own, w_out.shape[2] // nh), BF16)],
        scratch_shapes=[
            pltpu.VMEM(((nx - 1) * nz, blk, width), F32),
            pltpu.VMEM((nz - 1, blk, width), F32),
            pltpu.VMEM((nz - 1, blk, width), F32),
            pltpu.VMEM((blk, width), F32),
            pltpu.VMEM((nz - 1, nx * blk, width), F32),
            pltpu.VMEM((nx - 1, blk, width), F32),
            pltpu.VMEM((nx - 1, blk, width), F32),
            pltpu.VMEM((blk, width), F32),
            pltpu.VMEM((nrow - 1, own, 128), F32),
            pltpu.VMEM((own, heads * width), BF16),
            pltpu.VMEM((nh, own, w_out.shape[2] // nh), F32),
            pltpu.VMEM((nh - 1, own, w_out.shape[2] // nh), F32),
            dma((nx - 1) * nz), dma((nx - 1) * nz), dma(nz - 1), dma(nz - 1),
            dma(nz - 1), dma(nz - 1), dma(nx - 1), dma(nx - 1), dma(nrow - 1), dma(nrow - 1),
            dma(nx - 1), dma(nx - 1), dma(nx * (nz - 1)), dma(nx * (nz - 1)),
            dma(nz - 1), dma(nz - 1), dma((nx - 1) * nz), dma((nx - 1) * nz),
            dma(nh - 1), dma(nh - 1),
        ],
        compiler_params=pltpu.CompilerParams(
            collective_id=0, has_side_effects=True, vmem_limit_bytes=48 * 1024 * 1024
        ),
        name="exchange",
    )(
        rk, rq, stats, values.reshape(own, -1), zgate.reshape(own, -1), own_decay, own_beta,
        norm_gain.reshape(1, -1), w_out.reshape(-1, w_out.shape[2]),
    )

    new_state = pl.pallas_call(
        functools.partial(update_kernel, heads, depth),
        grid=(seqs // step,),
        in_specs=[row_spec, head_spec, head_spec, state_spec],
        out_specs=state_spec,
        out_shape=jax.ShapeDtypeStruct(flat.shape, F32),
        name="update",
    )(keys, decay_wide, delta, flat)
    return (layer_out, new_state.reshape(state.shape))


def solution(mesh):
    in_specs = (
        P(),
        P(None, "head", "row"),
        P(None, "head", "row"),
        P(None, "head", None),
        P(None, "head", None),
        P(None, "head"),
        P(None, "head"),
        P("head"),
        P("head"),
        P(),
        P("head", None, None),
        P(None, "head", "row", None),
    )
    out_specs = (P("row", "head"), P(None, "head", "row", None))
    return jax.shard_map(local, mesh=mesh, in_specs=in_specs, out_specs=out_specs, check_vma=False)
```

time: 326 us -> 191 us (0.59)
  Pallas kernels: 0 us -> 173 us
  waiting for transfers between devices: 134 us -> 0 us
  matrix products: 80.5 us -> 6.4 us
  blocking collectives: 57.3 us -> 0 us
  other arithmetic: 27.4 us -> 1.07 us
  between operations: 14.3 us -> 0.83 us
  local copies, waits for them, and re-layouts: 12.5 us -> 7.85 us
    pallas_call x0 -> x3, Pallas kernels: none -> 173 us  [the longest x1 115 us: local(): pl.pallas_call(functools.partial(exchange_kernel, nx, nz, nh, heads, grou...]
    psum x1 -> x0, waiting for transfers between devices: 134 us -> none  [local(): lax.psum((read_state(state, key_unit), read_state(state, query_unit), jnp...]
    dot_general x6 -> x7, matrix products: 78 us -> 6.4 us  [the longest x1 3.18 us: local(): jnp.einsum('bd,dhv->bhv', own_hidden, w_value, preferred_element_type=F32)]
    psum x2 -> x0, blocking collectives: 57.3 us -> none  [the longest x1 38.8 us: local(): lax.psum((jnp.sum(query * query, axis=-1), jnp.sum(keys * keys, axis=-1))...]
    add x1 -> x0, other arithmetic: 24.5 us -> none  [local(): decay[..., None, None] * state]
    reshape x1, local copies, waits for them, and re-layouts: 3.53 us -> 0.05 us  [local(): zgate.reshape(own, -1)]
    dot_general x2 -> x0, local copies, waits for them, and re-layouts: 3.41 us -> none  [read_state(): jnp.einsum('bhkv,bhk->bhv', source, widen(vector), precision=lax.Precisio...]
  transfers between devices with their start and end apart: 2 -> 0, of which waited for: 1 -> 0; matrix products, arithmetic and copies ran while one was open for 8% -> 0% of each run, Pallas kernels for 0% -> 0%
where the time goes in v1:
time: 191 us; the launch traced here: 189 us
  Pallas kernels  173 us (91%)
  local copies, waits for them, and re-layouts  7.85 us (4%)
  matrix products  6.4 us (3%)
    pallas_call x1, Pallas kernels, local(): pl.pallas_call(functools.partial(exchange_kernel, nx, nz, nh, heads, grou...  115 us
    pallas_call x1, Pallas kernels, local(): pl.pallas_call(functools.partial(update_kernel, heads, depth), grid=(seqs...  35.7 us
    pallas_call x1, Pallas kernels, local(): pl.pallas_call(functools.partial(read_kernel, heads, depth), grid=(seqs /...  22.2 us
    unnamed x23, local copies, waits for them, and re-layouts  4.61 us

profile of v1, /device:TPU:0, one launch (start us, length us, event | category | flops | bytes accessed | tf_op | source)
XLA Modules:
  0.0 189.5 jit_solution(17119594422782655182)
XLA Ops:
  0.6 0.0 copy-start
  0.7 0.8 exponential_negate_fusion
  1.5 0.8 copy-done
  2.2 0.0 copy-start.10
  2.2 3.2 %fusion.4 = f32[8,8,8,128]{3,2,1,0:T(8,128)S(1)} fusion(bf16[2048,8,128]{2,1,0:T(8,128)(2,1)} %param.15, bf16[512,2048]{1,0:T(8,128)(2,1)S(1)} %copy-done, s32[]{:T(128)S(6)} %select_n.54), kind=kOutput, calls=%fused_computation.5 | convolution fusion | flops 268435456 | bytes 4718596 | tf_op jit(solution)/shard_map/bd,dhv->bhv/dot_general | solution.py:330
  5.4 0.3 copy-done.10
  5.7 0.0 copy-start.7
  5.7 0.0 copy-start.8
  5.7 0.8 fusion.7
  6.5 0.0 copy-start.9
  6.6 0.0 copy-start.5
  6.6 0.0 copy-done.7
  6.6 0.0 copy-done.8
  6.6 0.0 copy-start.6
  6.7 0.7 convolution_bitcast_fusion.1
  7.3 0.0 copy-done.9
  7.4 0.2 fusion.52
  7.6 0.1 broadcast_in_dim.10
  7.8 0.0 copy-done.5
  7.8 0.0 copy-done.6
  7.9 0.7 convolution_bitcast_fusion
  8.6 0.3 fusion.21
  9.0 0.3 fusion.17
  9.3 0.3 fusion.19
  9.6 0.9 fusion.51
  10.5 0.1 copy.42
  10.7 1.9 %broadcast_in_dim.22.decay_ref = f32[4096,128]{1,0:T(8,128)} broadcast(f32[4096]{0:T(1024)S(1)} %broadcast_in_dim.10), dimensions={0} | broadcast | bytes 2113536 | tf_op jit(solution)/shard_map/broadcast_in_dim | solution.py:326
  12.6 0.0 copy-start.4
  12.6 22.2 %read.1 = (f32[4096,128]{1,0:T(8,128)}, f32[4096,128]{1,0:T(8,128)}) custom-call(f32[512,128]{1,0:T(8,128)} %get-tuple-element.11.q_ref, f32[512,128]{1,0:T(8,128)} %get-tuple-element.10.k_ref, f32[512,128,128]{2,1,0:T(8,128)} %bitcast.26), custom_call_target="tpu_custom_call" | custom-call | tf_op jit(solution)/shard_map/read/pallas_call | solution.py:339
  34.8 0.0 copy-done.4
  34.8 0.0 copy-start.3
  34.8 1.6 copy-done.3
  36.4 115.4 %exchange.1 = (f32[4096,128]{1,0:T(8,128)S(1)}, bf16[64,512]{1,0:T(8,128)(2,1)S(1)}) custom-call(f32[4096,128]{1,0:T(8,128)S(1)} %copy-done.3, f32[4096,128]{1,0:T(8,128)} %get-tuple-element.7.rq_ref, f32[512,128]{1,0:T(8,128)S(1)} %pad.4.stats_ref, f32[64,1024]{1,0:T(8,128)S(1)} %get-tuple-element.17.values_ref, ...), custom_call_target="tpu_custom_call" | custom-call | tf_op jit(solution)/shard_map/exchange/pallas_call | solution.py:351
  151.8 0.0 copy-start.2
  151.8 1.3 copy-done.2
  153.2 0.0 copy-start.1
  153.2 35.7 %update.1 = f32[512,128,128]{2,1,0:T(8,128)} custom-call(f32[512,128]{1,0:T(8,128)} %get-tuple-element.10.k_ref, f32[4096,128]{1,0:T(8,128)} %broadcast_in_dim.22.decay_ref, f32[4096,128]{1,0:T(8,128)} %copy-done.2, f32[512,128,128]{2,1,0:T(8,128)} %bitcast.27), custom_call_target="tpu_custom_call" | custom-call | tf_op jit(solution)/shard_map/update/pallas_call | solution.py:384
  188.9 0.6 copy.66
  189.5 0.0 copy-done.1
  (8 shorter events, 0.2 us)
Async XLA Ops:
  0.6 1.6 copy-start
  2.2 3.4 %copy-start.10 = (bf16[2048,8,128]{2,1,0:T(8,128)(2,1)S(1)}, bf16[2048,8,128]{2,1,0:T(8,128)(2,1)}, u32[]{:S(2)}) copy-start(bf16[2048,8,128]{2,1,0:T(8,128)(2,1)} %param.16) | copy-start | bytes 12582916
  5.7 0.9 copy-start.7
  5.7 0.9 copy-start.8
  6.5 0.8 copy-start.9
  6.6 1.2 copy-start.5
  6.6 1.2 copy-start.6
  12.6 22.2 %copy-start.4 = (f32[128]{0:T(128)S(1)}, f32[128]{0:T(128)}, u32[]{:S(2)}) copy-start(f32[128]{0:T(128)} %param.21) | copy-start | bytes 1540
  34.8 1.6 copy-start.3
  151.8 1.3 copy-start.2
  153.2 36.3 %copy-start.1 = (bf16[512,2048]{1,0:T(8,128)(2,1)S(1)}, bf16[512,2048]{1,0:T(8,128)(2,1)}, u32[]{:S(2)}) copy-start(bf16[512,2048]{1,0:T(8,128)(2,1)} %param.12) | copy-start | bytes 6291460
